TPU v7x, 32 devices: a whole 2x2x4 slice. The times are simulated.
32 devices in a mesh: grp: 2 (over y), seq: 16 (over z, x, core).
Axes of the slice: x: 2, y: 2, z: 4, core: 2. Of those that a mesh axis runs over, the one named last changes fastest.
Arguments:
- frames: bfloat16 [4, 10240, 1280], P('grp', 'seq'), parts along dimension 0, may hold values from -120 to 120
- dec_states: bfloat16 [2, 256, 1280], P(None, 'grp'), parts along dimension 1, may hold values from -6 to 6
- w_query: bfloat16 [1280, 1280], P(None, 'seq'), may hold values from -0.15625 to 0.15625
- w_keyval: bfloat16 [1280, 2560], replicated, may hold values from -0.15625 to 0.15625
- w_output: bfloat16 [1280, 1280], P(None, 'seq'), may hold values from -0.15625 to 0.15625
- head_slope: float32 [20], replicated, may hold values from 0.3 to 12
- lengths: int32 [4, 16], P('grp'), parts along dimension 0, may hold values from 128 to 640, as said below
- positions: int32 [2, 256], P(None, 'grp'), parts along dimension 1, may hold values from 0 to 15
Outputs:
- attended: bfloat16 [2, 256, 1280], P(None, 'grp', 'seq'), parts along dimension 1
There are 2 independent parts, one for each index of `grp`. A program takes and returns all parts, laid end to end along the dimension named above; an argument that names none is the same for every part. Nothing has to cross between parts.
Inputs may be any that keep to these rules, and one draw needn't show every extreme that they name: `lengths`: every step has one block of exactly 640 valid frames.
All inputs are finite; a program needn't handle non-finite values.
Results may differ from a plain program's by a relative error of at most 0.005.
The roundings to bfloat16 on the way count: a program that leaves them out, or rounds other values in their place, can miss the bound.
Values may be sent and summed in bfloat16 or wider, within the bound.
A program may use at most 128 MiB of HBM per device.

v0:
```python
import functools
import math
import jax
import jax.numpy as jnp
from jax import lax
from jax.sharding import PartitionSpec as P


def block_partial(
    queries,
    block_keys,
    block_values,
    length_now,
    slot_place,
    age_steps,
    row_positions,
    head_slope,
    devices,
):
    query_rows, head_count, head_size = queries.shape
    frame_count = block_keys.shape[0]
    keys_split = block_keys.reshape(frame_count, head_count, head_size)
    scores = jnp.einsum(
        "qhd,jhd->hqj", queries, keys_split, preferred_element_type=jnp.float32
    ) / math.sqrt(head_size)
    distance = (
        jnp.abs(row_positions.astype(jnp.float32) - slot_place.astype(jnp.float32)) / devices
        + age_steps
    )
    scores = scores - head_slope[:, None, None] * distance[None, :, None]
    valid = lax.broadcasted_iota(jnp.int32, (1, 1, frame_count), 2) < length_now
    scores = jnp.where(valid, scores, -jnp.inf)
    row_peak = jnp.max(scores, axis=2)
    weights = jnp.exp(scores - row_peak[:, :, None]).astype(jnp.bfloat16)
    row_total = jnp.sum(weights.astype(jnp.float32), axis=2)
    values_split = block_values.reshape(frame_count, head_count, head_size)
    row_context = jnp.einsum(
        "hqj,jhd->qhd", weights, values_split, preferred_element_type=jnp.float32
    )
    return (row_peak.T, row_total.T, row_context.reshape(query_rows, head_count * head_size))


def rescale(row_context, factors, head_count):
    query_rows = row_context.shape[0]
    spread_rows = row_context.reshape(query_rows, head_count, -1) * factors[:, :, None]
    return spread_rows.reshape(query_rows, -1)


def combine_parts(head_count, earlier, later):
    peak_one, total_one, context_one = earlier
    peak_two, total_two, context_two = later
    row_top = jnp.maximum(peak_one, peak_two)
    scale_one = jnp.exp(peak_one - row_top)
    scale_two = jnp.exp(peak_two - row_top)
    merged_total = total_one * scale_one + total_two * scale_two
    merged_context = rescale(context_one, scale_one, head_count) + rescale(
        context_two, scale_two, head_count
    )
    return (row_top, merged_total, merged_context)


def local(frames, dec_states, w_query, w_keyval, w_output, head_slope, lengths, positions):
    devices = lax.axis_size("seq")
    own_index = lax.axis_index("seq")
    step_count, frame_count, model_width = frames.shape
    query_rows = dec_states.shape[1]
    head_count = head_slope.shape[0]
    head_size = model_width // head_count
    frame_rows = frames.reshape(step_count * frame_count, model_width)
    keyval = jnp.dot(frame_rows, w_keyval, preferred_element_type=jnp.float32).astype(jnp.bfloat16)
    block_keys = keyval[:, :model_width].reshape(step_count, frame_count, model_width)
    block_values = keyval[:, model_width:].reshape(step_count, frame_count, model_width)
    dec_rows = dec_states.reshape(step_count * query_rows, model_width)
    local_query = jnp.dot(dec_rows, w_query, preferred_element_type=jnp.float32).astype(
        jnp.bfloat16
    )
    queries = lax.all_gather(local_query, "seq", axis=1, tiled=True)
    queries = queries.reshape(step_count, query_rows, head_count, head_size)
    combine = functools.partial(combine_parts, head_count)
    slot_place = (own_index + 1) % devices
    results = []
    for step_now in range(step_count):
        running = None
        for older_step in range(step_now + 1):
            partial_now = block_partial(
                queries[step_now],
                block_keys[older_step],
                block_values[older_step],
                lengths[older_step, own_index],
                slot_place,
                float(step_now - older_step),
                positions[step_now],
                head_slope,
                devices,
            )
            running = partial_now if running is None else combine(running, partial_now)
        row_peak, row_total, row_context = running
        row_top = lax.pmax(row_peak, "seq")
        factors = jnp.exp(row_peak - row_top)
        row_total, row_context = lax.psum(
            (row_total * factors, rescale(row_context, factors, head_count)), "seq"
        )
        context = row_context.reshape(query_rows, head_count, head_size) / row_total[:, :, None]
        context = context.reshape(query_rows, model_width).astype(jnp.bfloat16)
        results.append(
            jnp.dot(context, w_output, preferred_element_type=jnp.float32).astype(jnp.bfloat16)
        )
    return jnp.stack(results)


def solution(mesh):
    return jax.shard_map(
        local,
        mesh=mesh,
        in_specs=(
            P("grp", "seq", None),
            P(None, "grp", None),
            P(None, "seq"),
            P(),
            P(None, "seq"),
            P(),
            P("grp", None),
            P(None, "grp"),
        ),
        out_specs=P(None, "grp", "seq"),
        check_vma=False,
    )
```

profile of v0, /device:TPU:0, one launch (start us, length us, event | category | flops | bytes accessed | tf_op | source)
XLA Modules:
  0.0 259.9 jit_solution(2014881977530584230)
XLA Ops:
  8.2 1.4 constant_dynamic-slice_fusion.1
  10.3 10.8 %convolution_convert_fusion = bf16[1280,2560]{1,0:T(8,128)(2,1)S(1)} fusion(bf16[1280,1280]{1,0:T(8,128)(2,1)S(1)} %bitcast.89, bf16[1280,2560]{1,0:T(8,128)(2,1)} %param.11), kind=kOutput, calls=%fused_computation | convolution fusion | flops 8391884800 | bytes 16384000 | tf_op jit(solution)/shard_map/dot_general | solution.py:70
  21.1 2.8 %fusion.18 = (bf16[640,1280]{1,0:T(8,128)(2,1)}, bf16[640,1280]{1,0:T(8,128)(2,1)}, bf16[640,1280]{1,0:T(8,128)(2,1)}, bf16[640,1280]{1,0:T(8,128)(2,1)}) fusion(bf16[1280,2560]{1,0:T(8,128)(2,1)S(1)} %convolution_convert_fusion), kind=kLoop, calls=%fused_computation.53 | loop fusion | bytes 13107200 | tf_op jit(solution)/shard_map/slice | solution.py:88
  23.9 3.5 %copy.16 = bf16[640,1280]{0,1:T(8,128)(2,1)} copy(bf16[640,1280]{1,0:T(8,128)(2,1)} %get-tuple-element.26) | data formatting | bytes 3276800 | tf_op jit(solution)/shard_map/slice | solution.py:87
  27.4 1.4 convolution_convert_fusion.1
  28.9 25.1 %all_gather.3 = bf16[256,1280]{0,1:T(8,128)(2,1)S(1)} all-gather(bf16[256,80]{0,1:T(8,128)(2,1)S(1)} %convolution_convert_fusion.1), channel_id=1, replica_groups=mesh['grp'=2,'seq'=16] {'seq'}, dimensions={1}, use_global_device_ids=true | all-gather | bytes 696320 | tf_op jit(solution)/shard_map/all_gather | solution.py:77
  54.0 0.9 fusion.19
  55.5 3.5 %copy.17 = bf16[640,1280]{0,1:T(8,128)(2,1)} copy(bf16[640,1280]{1,0:T(8,128)(2,1)} %get-tuple-element.25) | data formatting | bytes 3276800 | tf_op jit(solution)/shard_map/slice | solution.py:87
  59.1 2.7 %fusion.20 = f32[20,128,640]{2,1,0:T(8,128)S(1)} fusion(bf16[128,20,64]{0,2,1:T(8,128)(2,1)} %bitcast.98, bf16[640,20,64]{0,2,1:T(8,128)(2,1)} %bitcast.92), kind=kOutput, calls=%fused_computation.55 | convolution fusion | flops 209715200 | bytes 8519680 | tf_op jit(solution)/shard_map/qhd,jhd->hqj/dot_general | solution.py:23
  61.9 1.6 fusion.2
  63.5 1.0 copy-done.3
  64.8 4.6 %fusion = (f32[20,128]{1,0:T(8,128)S(1)}, f32[20,128]{1,0:T(8,128)S(1)}, f32[20,128,640]{2,1,0:T(8,128)}) fusion(f32[20,128]{1,0:T(8,128)S(1)} %get-tuple-element.33, pred[640]{0:T(1024)(128)(4,1)S(1)} %iota_compare_fusion.1, f32[20,128]{1,0:T(8,128)S(1)} %get-tuple-element.31, f32[20,128,640]{2,1,0:T(8,128)S(1)} %fusion.20, ...), kind=kOutput, calls=%fused_computation.10 | convolution fusion | flops 222817280 | bytes 15114880 | tf_op jit(solution)/shard_map/qhd,jhd->hqj/dot_general | solution.py:23
  69.4 2.0 convert_reduce_fusion
  71.4 3.5 %copy.15 = bf16[640,1280]{0,1:T(8,128)(2,1)} copy(bf16[640,1280]{1,0:T(8,128)(2,1)} %get-tuple-element.23) | data formatting | bytes 3276800 | tf_op jit(solution)/shard_map/slice | solution.py:88
  74.9 3.5 %copy.18 = bf16[640,1280]{0,1:T(8,128)(2,1)} copy(bf16[640,1280]{1,0:T(8,128)(2,1)} %get-tuple-element.24) | data formatting | bytes 3276800 | tf_op jit(solution)/shard_map/slice | solution.py:88
  78.4 7.1 %convert_reduce_fusion.2 = (f32[20,128]{1,0:T(8,128)S(1)}, f32[20,128]{1,0:T(8,128)S(1)}) fusion(f32[20,128]{1,0:T(8,128)S(1)} %get-tuple-element.7, f32[20,128]{1,0:T(8,128)S(1)} %get-tuple-element.33, f32[20,128,640]{2,1,0:T(8,128)} %get-tuple-element.36, pred[640]{0:T(1024)(128)(4,1)S(1)} %iota_compare_fusion.1, f32[20,128]{1,0:T(8,128)S(1)} %get-tuple-element.8, ...), kind=kLoop, calls=%fused_computation.7 | loop fusion | flops 22932480 | bytes 13169280 | tf_op jit(solution)/shard_map/reduce_sum | solution.py:35
  85.5 57.8 %all-reduce.2 = (f32[128,20]{0,1:T(8,128)S(1)}, f32[128,20]{0,1:T(8,128)S(1)}) all-reduce(f32[128,20]{0,1:T(8,128)S(1)} %bitcast_maximum_fusion, f32[128,20]{0,1:T(8,128)S(1)} %bitcast.104), channel_id=1, replica_groups=mesh['grp'=2,'seq'=16] {'seq'}, use_global_device_ids=true, to_apply=%region_7.8 | all-reduce | flops 5120 | bytes 40960 | tf_op jit(solution)/shard_map/pmax | solution.py:98
  143.4 6.2 %fusion.3 = f32[128,20,64]{0,2,1:T(8,128)} fusion(bf16[640,20,64]{0,2,1:T(8,128)(2,1)} %bitcast.94, f32[128,20]{0,1:T(8,128)S(1)} %get-tuple-element.38, f32[20,128,640]{2,1,0:T(8,128)} %get-tuple-element.36, f32[20,128]{1,0:T(8,128)S(1)} %get-tuple-element.7, f32[20,128]{1,0:T(8,128)S(1)} %get-tuple-element.33, pred[640]{0:T(1024)(128)(4,1)S(1)} %iota_compare_fusion.1), kind=kOutput, calls=%fused_computation.16 | convolution fusion | flops 218071040 | bytes 8878720 | tf_op jit(solution)/shard_map/hqj,jhd->qhd/dot_general | solution.py:37
  149.6 4.3 %fusion.7 = f32[128,20,64]{0,2,1:T(8,128)S(1)} fusion(bf16[640,20,64]{0,2,1:T(8,128)(2,1)S(1)} %bitcast.96, f32[128,20]{0,1:T(8,128)S(1)} %get-tuple-element.20, f32[20,128,640]{2,1,0:T(8,128)} %copy-done.2, f32[20,128]{1,0:T(8,128)S(1)} %get-tuple-element.34, f32[20,128]{1,0:T(8,128)S(1)} %get-tuple-element.32, pred[640]{0:T(1024)(128)(4,1)S(1)} %iota_compare_fusion), kind=kOutput, calls=%fused_computation.20 | convolution fusion | flops 218071040 | bytes 8878720 | tf_op jit(solution)/shard_map/hqj,jhd->qhd/dot_general | solution.py:37
  154.9 2.9 %fusion.6 = f32[128,20,64]{0,2,1:T(8,128)} fusion(f32[128,20,64]{0,2,1:T(8,128)S(1)} %fusion.7, bf16[640,20,64]{0,2,1:T(8,128)(2,1)S(1)} %bitcast.95, f32[128,20]{0,1:T(8,128)S(1)} %get-tuple-element.19, f32[128,20]{0,1:T(8,128)S(1)} %get-tuple-element.18, f32[20,128,640]{2,1,0:T(8,128)S(1)} %bitcast.91, f32[20,128]{1,0:T(8,128)S(1)} %get-tuple-element.8, ...), kind=kOutput, calls=%fused_computation.19 | convolution fusion | flops 218398720 | bytes 9544320 | tf_op jit(solution)/shard_map/hqj,jhd->qhd/dot_general | solution.py:37
  157.9 58.0 %all-reduce = (f32[128,20]{0,1:T(8,128)S(1)}, f32[128,20]{0,1:T(8,128)S(1)}) all-reduce(f32[128,20]{0,1:T(8,128)S(1)} %get-tuple-element.17, f32[128,20]{0,1:T(8,128)S(1)} %get-tuple-element.37), channel_id=1, replica_groups=mesh['grp'=2,'seq'=16] {'seq'}, use_global_device_ids=true, to_apply=%region_11.12 | all-reduce | flops 5120 | bytes 40960 | tf_op jit(solution)/shard_map/psum | solution.py:100
  215.9 33.8 %all-reduce.5.cloned.1.call-done = (f32[128,1280]{0,1:T(8,128)}, f32[128,1280]{0,1:T(8,128)}) async-done(((f32[128,1280]{0,1:T(8,128)}, f32[128,1280]{0,1:T(8,128)}), (f32[128,1280]{0,1:T(8,128)}, f32[128,1280]{0,1:T(8,128)})) %all-reduce.5.cloned.1.call-update) | async-done | bytes 1310736 | tf_op jit(solution)/shard_map/psum | solution.py:100
  249.7 1.1 fusion.11
  251.0 1.1 fusion.10
  (40 shorter events, 5.5 us)
Async XLA Ops:
  6.5 3.7 %copy-start = (bf16[2,640,1280]{2,1,0:T(8,128)(2,1)S(1)}, bf16[2,640,1280]{2,1,0:T(8,128)(2,1)}, u32[]{:S(2)}) copy-start(bf16[2,640,1280]{2,1,0:T(8,128)(2,1)} %param.8) | copy-start | bytes 9830404
  6.5 243.1 %all-reduce.5.cloned.1.call-start = ((), (), s32[]{:S(2)}) async-start(), calls=%async_computation | async-start | bytes 2621440 | tf_op jit(solution)/shard_map/psum | solution.py:100
  21.1 6.3 %copy-start.10 = (bf16[1280,80]{0,1:T(8,128)(2,1)S(1)}, bf16[1280,80]{0,1:T(8,128)(2,1)}, u32[]{:S(2)}) copy-start(bf16[1280,80]{0,1:T(8,128)(2,1)} %param.10) | copy-start | bytes 614404
  54.0 7.9 %copy-start.11 = (f32[20]{0:T(128)S(1)}, f32[20]{0:T(128)}, u32[]{:S(2)}) copy-start(f32[20]{0:T(128)} %param.13) | copy-start | bytes 244
  59.1 2.9 %copy-start.6 = (bf16[640,1280]{0,1:T(8,128)(2,1)S(1)}, bf16[640,1280]{0,1:T(8,128)(2,1)}, u32[]{:S(2)}) copy-start(bf16[640,1280]{0,1:T(8,128)(2,1)} %copy.17) | copy-start | bytes 4915204
  59.1 2.9 %copy-start.7 = (bf16[128,1280]{0,1:T(8,128)(2,1)S(1)}, bf16[128,1280]{0,1:T(8,128)(2,1)}, u32[]{:S(2)}) copy-start(bf16[128,1280]{0,1:T(8,128)(2,1)} %get-tuple-element.28) | copy-start | bytes 983044
  61.8 7.5 %copy-start.1 = (f32[20,128,640]{2,1,0:T(8,128)}, f32[20,128,640]{2,1,0:T(8,128)S(1)}, u32[]{:S(2)}) copy-start(f32[20,128,640]{2,1,0:T(8,128)S(1)} %fusion.20) | copy-start | bytes 19660804
  61.8 2.6 %copy-start.3 = (bf16[640,1280]{0,1:T(8,128)(2,1)S(1)}, bf16[640,1280]{0,1:T(8,128)(2,1)}, u32[]{:S(2)}) copy-start(bf16[640,1280]{0,1:T(8,128)(2,1)} %copy.16) | copy-start | bytes 4915204
  61.8 2.9 %copy-start.9 = (bf16[128,1280]{0,1:T(8,128)(2,1)S(1)}, bf16[128,1280]{0,1:T(8,128)(2,1)}, u32[]{:S(2)}) copy-start(bf16[128,1280]{0,1:T(8,128)(2,1)} %get-tuple-element.27) | copy-start | bytes 983044
  63.5 5.9 %copy-start.2 = (f32[20,128,640]{2,1,0:T(8,128)}, f32[20,128,640]{2,1,0:T(8,128)S(1)}, u32[]{:S(2)}) copy-start(f32[20,128,640]{2,1,0:T(8,128)S(1)} %get-tuple-element.35) | copy-start | bytes 19660804
  143.3 6.3 %copy-start.5 = (bf16[640,1280]{0,1:T(8,128)(2,1)S(1)}, bf16[640,1280]{0,1:T(8,128)(2,1)}, u32[]{:S(2)}) copy-start(bf16[640,1280]{0,1:T(8,128)(2,1)} %copy.18) | copy-start | bytes 4915204
  149.6 4.3 %slice-start = ((s8[6553600]{0:T(1024)(128)(4,1)}), s8[4194304]{0:T(1024)(128)(4,1)S(1)}, s32[]{:S(2)}) async-start(s8[6553600]{0:T(1024)(128)(4,1)} %bitcast.90), calls=%async_computation.1 | async-start | bytes 8388608
  149.6 4.6 %copy-start.4 = (bf16[640,1280]{0,1:T(8,128)(2,1)S(1)}, bf16[640,1280]{0,1:T(8,128)(2,1)}, u32[]{:S(2)}) copy-start(bf16[640,1280]{0,1:T(8,128)(2,1)} %copy.15) | copy-start | bytes 4915204
  149.6 5.3 %slice-start.1 = ((s8[6553600]{0:T(1024)(128)(4,1)}), s8[2359296]{0:T(1024)(128)(4,1)S(1)}, s32[]{:S(2)}) async-start(s8[6553600]{0:T(1024)(128)(4,1)} %bitcast.90), calls=%async_computation.2 | async-start | bytes 4718592
  154.9 95.9 %copy-start.8 = (bf16[1280,80]{0,1:T(8,128)(2,1)S(1)}, bf16[1280,80]{0,1:T(8,128)(2,1)}, u32[]{:S(2)}) copy-start(bf16[1280,80]{0,1:T(8,128)(2,1)} %param.12) | copy-start | bytes 614404
Sparse Core Ops, SparseCore 0:
  158.0 91.5 all-reduce.4
where the time goes:
time: 260 us
  blocking collectives  141 us (54%)
  matrix products  35 us (13%)
  waiting for transfers between devices  33.8 us (13%)
  local copies, waits for them, and re-layouts  21.6 us (8%)
  other arithmetic  15.1 us (6%)
  between operations  13.6 us (5%)
    psum x1, blocking collectives, local(): lax.psum((row_total * factors, rescale(row_context, factors, head_count))...  58 us
    pmax x1, blocking collectives, local(): row_top = lax.pmax(row_peak, 'seq')  57.8 us
    psum x1, waiting for transfers between devices, local(): lax.psum((row_total * factors, rescale(row_context, factors, head_count))...  33.8 us
    all_gather x1, blocking collectives, local(): queries = lax.all_gather(local_query, 'seq', axis=1, tiled=True)  25.1 us
    dot_general x3, matrix products, block_partial(): jnp.einsum('hqj,jhd->qhd', weights, values_split, preferred_element_type=...  13.5 us
    dot_general x1, matrix products, local(): jnp.dot(frame_rows, w_keyval, preferred_element_type=jnp.float32)  10.8 us
    slice x3, local copies, waits for them, and re-layouts, local(): block_values[older_step]  9.87 us
    reduce_sum x2, other arithmetic, block_partial(): row_total = jnp.sum(weights.astype(jnp.float32), axis=2)  9.08 us
  transfers between devices with their start and end apart: 1, of which 1 were waited for; matrix products, arithmetic and copies ran while one was open for 0% of the time, Pallas kernels for 0%

commit v1 on v0

--- a/solution.py
+++ b/solution.py
@@ -74,7 +74,7 @@
     local_query = jnp.dot(dec_rows, w_query, preferred_element_type=jnp.float32).astype(
         jnp.bfloat16
     )
-    queries = lax.all_gather(local_query, "seq", axis=1, tiled=True)
+    queries = jnp.concatenate(lax.all_gather(local_query, "seq"), axis=1)
     queries = queries.reshape(step_count, query_rows, head_count, head_size)
     combine = functools.partial(combine_parts, head_count)
     slot_place = (own_index + 1) % devices

time: 260 us -> 262 us (level)
  no operation moved by 1% of the time
where the time goes in v1:
time: 262 us; the launch traced here: 261 us
  blocking collectives  141 us (54%)
  matrix products  35 us (13%)
  waiting for transfers between devices  33.8 us (13%)
  local copies, waits for them, and re-layouts  22.5 us (9%)
  other arithmetic  15.1 us (6%)
  between operations  13.6 us (5%)
    psum x1, blocking collectives, local(): lax.psum((row_total * factors, rescale(row_context, factors, head_count))...  58 us
    pmax x1, blocking collectives, local(): row_top = lax.pmax(row_peak, 'seq')  57.8 us
    psum x1, waiting for transfers between devices, local(): lax.psum((row_total * factors, rescale(row_context, factors, head_count))...  33.8 us
    all_gather x1, blocking collectives, local(): queries = jnp.concatenate(lax.all_gather(local_query, 'seq'), axis=1)  25.3 us
    dot_general x3, matrix products, block_partial(): jnp.einsum('hqj,jhd->qhd', weights, values_split, preferred_element_type=...  13.5 us
    dot_general x1, matrix products, local(): jnp.dot(frame_rows, w_keyval, preferred_element_type=jnp.float32)  10.8 us
    slice x3, local copies, waits for them, and re-layouts, local(): block_values[older_step]  9.87 us
    reduce_sum x2, other arithmetic, block_partial(): row_total = jnp.sum(weights.astype(jnp.float32), axis=2)  9.08 us
  transfers between devices with their start and end apart: 1, of which 1 were waited for; matrix products, arithmetic and copies ran while one was open for 0% of the time, Pallas kernels for 0%

profile of v1, /device:TPU:0, one launch (start us, length us, event | category | flops | bytes accessed | tf_op | source)
XLA Modules:
  0.0 261.0 jit_solution(10012711353919975479)
XLA Ops:
  7.4 0.8 multiply_bitcast_fusion.1
  8.2 1.4 constant_dynamic-slice_fusion.1
  10.3 10.8 %convolution_convert_fusion = bf16[1280,2560]{1,0:T(8,128)(2,1)S(1)} fusion(bf16[1280,1280]{1,0:T(8,128)(2,1)S(1)} %bitcast.95, bf16[1280,2560]{1,0:T(8,128)(2,1)} %param.11), kind=kOutput, calls=%fused_computation | convolution fusion | flops 8391884800 | bytes 16384000 | tf_op jit(solution)/shard_map/dot_general | solution.py:70
  21.1 2.8 %fusion.18 = (bf16[640,1280]{1,0:T(8,128)(2,1)}, bf16[640,1280]{1,0:T(8,128)(2,1)}, bf16[640,1280]{1,0:T(8,128)(2,1)}, bf16[640,1280]{1,0:T(8,128)(2,1)}) fusion(bf16[1280,2560]{1,0:T(8,128)(2,1)S(1)} %convolution_convert_fusion), kind=kLoop, calls=%fused_computation.53 | loop fusion | bytes 13107200 | tf_op jit(solution)/shard_map/slice | solution.py:88
  23.9 3.5 %copy.19 = bf16[640,1280]{0,1:T(8,128)(2,1)} copy(bf16[640,1280]{1,0:T(8,128)(2,1)} %get-tuple-element.26) | data formatting | bytes 3276800 | tf_op jit(solution)/shard_map/slice | solution.py:87
  27.4 1.4 convolution_convert_fusion.1
  28.9 25.3 %all-gather = bf16[4096,80]{0,1:T(8,128)(2,1)S(1)} all-gather(bf16[256,80]{0,1:T(8,128)(2,1)S(1)} %convolution_convert_fusion.1), channel_id=2, replica_groups=mesh['grp'=2,'seq'=16] {'seq'}, dimensions={0}, use_global_device_ids=true | all-gather | bytes 696320 | tf_op jit(solution)/shard_map/all_gather | solution.py:77
  56.7 3.5 %copy.21 = bf16[640,1280]{0,1:T(8,128)(2,1)} copy(bf16[640,1280]{1,0:T(8,128)(2,1)} %get-tuple-element.25) | data formatting | bytes 3276800 | tf_op jit(solution)/shard_map/slice | solution.py:87
  60.2 2.7 %fusion.20 = f32[20,128,640]{2,1,0:T(8,128)S(1)} fusion(bf16[128,20,64]{0,2,1:T(8,128)(2,1)} %bitcast.106, bf16[640,20,64]{0,2,1:T(8,128)(2,1)} %bitcast.98), kind=kOutput, calls=%fused_computation.55 | convolution fusion | flops 209715200 | bytes 8519680 | tf_op jit(solution)/shard_map/qhd,jhd->hqj/dot_general | solution.py:23
  63.1 1.6 fusion.2
  64.7 1.0 copy-done.3
  65.9 4.6 %fusion = (f32[20,128]{1,0:T(8,128)S(1)}, f32[20,128]{1,0:T(8,128)S(1)}, f32[20,128,640]{2,1,0:T(8,128)}) fusion(f32[20,128]{1,0:T(8,128)S(1)} %get-tuple-element.33, pred[640]{0:T(1024)(128)(4,1)S(1)} %iota_compare_fusion.1, f32[20,128]{1,0:T(8,128)S(1)} %get-tuple-element.31, f32[20,128,640]{2,1,0:T(8,128)S(1)} %fusion.20, ...), kind=kOutput, calls=%fused_computation.10 | convolution fusion | flops 222817280 | bytes 15114880 | tf_op jit(solution)/shard_map/qhd,jhd->hqj/dot_general | solution.py:23
  70.5 2.0 convert_reduce_fusion
  72.6 3.5 %copy.17 = bf16[640,1280]{0,1:T(8,128)(2,1)} copy(bf16[640,1280]{1,0:T(8,128)(2,1)} %get-tuple-element.23) | data formatting | bytes 3276800 | tf_op jit(solution)/shard_map/slice | solution.py:88
  76.1 3.5 %copy.22 = bf16[640,1280]{0,1:T(8,128)(2,1)} copy(bf16[640,1280]{1,0:T(8,128)(2,1)} %get-tuple-element.24) | data formatting | bytes 3276800 | tf_op jit(solution)/shard_map/slice | solution.py:88
  79.6 7.1 %convert_reduce_fusion.2 = (f32[20,128]{1,0:T(8,128)S(1)}, f32[20,128]{1,0:T(8,128)S(1)}) fusion(f32[20,128]{1,0:T(8,128)S(1)} %get-tuple-element.7, f32[20,128]{1,0:T(8,128)S(1)} %get-tuple-element.33, f32[20,128,640]{2,1,0:T(8,128)} %get-tuple-element.36, pred[640]{0:T(1024)(128)(4,1)S(1)} %iota_compare_fusion.1, f32[20,128]{1,0:T(8,128)S(1)} %get-tuple-element.8, ...), kind=kLoop, calls=%fused_computation.7 | loop fusion | flops 22932480 | bytes 13169280 | tf_op jit(solution)/shard_map/reduce_sum | solution.py:35
  86.7 57.8 %all-reduce.2 = (f32[128,20]{0,1:T(8,128)S(1)}, f32[128,20]{0,1:T(8,128)S(1)}) all-reduce(f32[128,20]{0,1:T(8,128)S(1)} %bitcast_maximum_fusion, f32[128,20]{0,1:T(8,128)S(1)} %bitcast.112), channel_id=1, replica_groups=mesh['grp'=2,'seq'=16] {'seq'}, use_global_device_ids=true, to_apply=%region_7.8 | all-reduce | flops 5120 | bytes 40960 | tf_op jit(solution)/shard_map/pmax | solution.py:98
  144.5 6.2 %fusion.3 = f32[128,20,64]{0,2,1:T(8,128)} fusion(bf16[640,20,64]{0,2,1:T(8,128)(2,1)} %bitcast.102, f32[128,20]{0,1:T(8,128)S(1)} %get-tuple-element.38, f32[20,128,640]{2,1,0:T(8,128)} %get-tuple-element.36, f32[20,128]{1,0:T(8,128)S(1)} %get-tuple-element.7, f32[20,128]{1,0:T(8,128)S(1)} %get-tuple-element.33, pred[640]{0:T(1024)(128)(4,1)S(1)} %iota_compare_fusion.1), kind=kOutput, calls=%fused_computation.16 | convolution fusion | flops 218071040 | bytes 8878720 | tf_op jit(solution)/shard_map/hqj,jhd->qhd/dot_general | solution.py:37
  150.8 4.3 %fusion.7 = f32[128,20,64]{0,2,1:T(8,128)S(1)} fusion(bf16[640,20,64]{0,2,1:T(8,128)(2,1)S(1)} %bitcast.104, f32[128,20]{0,1:T(8,128)S(1)} %get-tuple-element.20, f32[20,128,640]{2,1,0:T(8,128)} %copy-done.2, f32[20,128]{1,0:T(8,128)S(1)} %get-tuple-element.34, f32[20,128]{1,0:T(8,128)S(1)} %get-tuple-element.32, pred[640]{0:T(1024)(128)(4,1)S(1)} %iota_compare_fusion), kind=kOutput, calls=%fused_computation.20 | convolution fusion | flops 218071040 | bytes 8878720 | tf_op jit(solution)/shard_map/hqj,jhd->qhd/dot_general | solution.py:37
  156.1 2.9 %fusion.6 = f32[128,20,64]{0,2,1:T(8,128)} fusion(f32[128,20,64]{0,2,1:T(8,128)S(1)} %fusion.7, bf16[640,20,64]{0,2,1:T(8,128)(2,1)S(1)} %bitcast.103, f32[128,20]{0,1:T(8,128)S(1)} %get-tuple-element.19, f32[128,20]{0,1:T(8,128)S(1)} %get-tuple-element.18, f32[20,128,640]{2,1,0:T(8,128)S(1)} %bitcast.97, f32[20,128]{1,0:T(8,128)S(1)} %get-tuple-element.8, ...), kind=kOutput, calls=%fused_computation.19 | convolution fusion | flops 218398720 | bytes 9544320 | tf_op jit(solution)/shard_map/hqj,jhd->qhd/dot_general | solution.py:37
  159.1 58.0 %all-reduce = (f32[128,20]{0,1:T(8,128)S(1)}, f32[128,20]{0,1:T(8,128)S(1)}) all-reduce(f32[128,20]{0,1:T(8,128)S(1)} %get-tuple-element.17, f32[128,20]{0,1:T(8,128)S(1)} %get-tuple-element.37), channel_id=1, replica_groups=mesh['grp'=2,'seq'=16] {'seq'}, use_global_device_ids=true, to_apply=%region_11.12 | all-reduce | flops 5120 | bytes 40960 | tf_op jit(solution)/shard_map/psum | solution.py:100
  217.1 33.8 %all-reduce.5.cloned.1.call-done = (f32[128,1280]{0,1:T(8,128)}, f32[128,1280]{0,1:T(8,128)}) async-done(((f32[128,1280]{0,1:T(8,128)}, f32[128,1280]{0,1:T(8,128)}), (f32[128,1280]{0,1:T(8,128)}, f32[128,1280]{0,1:T(8,128)})) %all-reduce.5.cloned.1.call-update) | async-done | bytes 1310736 | tf_op jit(solution)/shard_map/psum | solution.py:100
  250.8 1.1 fusion.11
  252.2 1.1 fusion.10
  (43 shorter events, 6.5 us)
Async XLA Ops:
  6.5 3.7 %copy-start = (bf16[2,640,1280]{2,1,0:T(8,128)(2,1)S(1)}, bf16[2,640,1280]{2,1,0:T(8,128)(2,1)}, u32[]{:S(2)}) copy-start(bf16[2,640,1280]{2,1,0:T(8,128)(2,1)} %param.8) | copy-start | bytes 9830404
  6.5 244.3 %all-reduce.5.cloned.1.call-start = ((), (), s32[]{:S(2)}) async-start(), calls=%async_computation | async-start | bytes 2621440 | tf_op jit(solution)/shard_map/psum | solution.py:100
  21.1 6.3 %copy-start.10 = (bf16[1280,80]{0,1:T(8,128)(2,1)S(1)}, bf16[1280,80]{0,1:T(8,128)(2,1)}, u32[]{:S(2)}) copy-start(bf16[1280,80]{0,1:T(8,128)(2,1)} %param.10) | copy-start | bytes 614404
  54.4 8.6 %copy-start.11 = (f32[20]{0:T(128)S(1)}, f32[20]{0:T(128)}, u32[]{:S(2)}) copy-start(f32[20]{0:T(128)} %param.13) | copy-start | bytes 244
  60.2 2.9 %copy-start.6 = (bf16[640,1280]{0,1:T(8,128)(2,1)S(1)}, bf16[640,1280]{0,1:T(8,128)(2,1)}, u32[]{:S(2)}) copy-start(bf16[640,1280]{0,1:T(8,128)(2,1)} %copy.21) | copy-start | bytes 4915204
  60.2 2.9 %copy-start.7 = (bf16[128,16,80]{0,2,1:T(8,128)(2,1)S(1)}, bf16[128,16,80]{0,2,1:T(8,128)(2,1)}, u32[]{:S(2)}) copy-start(bf16[128,16,80]{0,2,1:T(8,128)(2,1)} %copy.20) | copy-start | bytes 983044
  63.0 7.5 %copy-start.1 = (f32[20,128,640]{2,1,0:T(8,128)}, f32[20,128,640]{2,1,0:T(8,128)S(1)}, u32[]{:S(2)}) copy-start(f32[20,128,640]{2,1,0:T(8,128)S(1)} %fusion.20) | copy-start | bytes 19660804
  63.0 2.6 %copy-start.3 = (bf16[640,1280]{0,1:T(8,128)(2,1)S(1)}, bf16[640,1280]{0,1:T(8,128)(2,1)}, u32[]{:S(2)}) copy-start(bf16[640,1280]{0,1:T(8,128)(2,1)} %copy.19) | copy-start | bytes 4915204
  63.0 2.9 %copy-start.9 = (bf16[128,16,80]{0,2,1:T(8,128)(2,1)S(1)}, bf16[128,16,80]{0,2,1:T(8,128)(2,1)}, u32[]{:S(2)}) copy-start(bf16[128,16,80]{0,2,1:T(8,128)(2,1)} %copy.18) | copy-start | bytes 983044
  64.7 5.9 %copy-start.2 = (f32[20,128,640]{2,1,0:T(8,128)}, f32[20,128,640]{2,1,0:T(8,128)S(1)}, u32[]{:S(2)}) copy-start(f32[20,128,640]{2,1,0:T(8,128)S(1)} %get-tuple-element.35) | copy-start | bytes 19660804
  144.5 6.3 %copy-start.5 = (bf16[640,1280]{0,1:T(8,128)(2,1)S(1)}, bf16[640,1280]{0,1:T(8,128)(2,1)}, u32[]{:S(2)}) copy-start(bf16[640,1280]{0,1:T(8,128)(2,1)} %copy.22) | copy-start | bytes 4915204
  150.8 4.3 %slice-start = ((s8[6553600]{0:T(1024)(128)(4,1)}), s8[4194304]{0:T(1024)(128)(4,1)S(1)}, s32[]{:S(2)}) async-start(s8[6553600]{0:T(1024)(128)(4,1)} %bitcast.96), calls=%async_computation.1 | async-start | bytes 8388608
  150.8 4.6 %copy-start.4 = (bf16[640,1280]{0,1:T(8,128)(2,1)S(1)}, bf16[640,1280]{0,1:T(8,128)(2,1)}, u32[]{:S(2)}) copy-start(bf16[640,1280]{0,1:T(8,128)(2,1)} %copy.17) | copy-start | bytes 4915204
  150.8 5.3 %slice-start.1 = ((s8[6553600]{0:T(1024)(128)(4,1)}), s8[2359296]{0:T(1024)(128)(4,1)S(1)}, s32[]{:S(2)}) async-start(s8[6553600]{0:T(1024)(128)(4,1)} %bitcast.96), calls=%async_computation.2 | async-start | bytes 4718592
  156.1 95.9 %copy-start.8 = (bf16[1280,80]{0,1:T(8,128)(2,1)S(1)}, bf16[1280,80]{0,1:T(8,128)(2,1)}, u32[]{:S(2)}) copy-start(bf16[1280,80]{0,1:T(8,128)(2,1)} %param.12) | copy-start | bytes 614404
Sparse Core Ops, SparseCore 0:
  159.2 91.5 all-reduce.4
